TPU v7x, 32 devices: a whole 2x2x4 slice. The times are simulated.
32 devices in a mesh: rep: 4 (over x, core), fsdp: 8 (over z, y).
Axes of the slice: x: 2, y: 2, z: 4, core: 2. Of those that a mesh axis runs over, the one named last changes fastest.
Arguments:
- features: bfloat16 [4096, 1280], P(('rep', 'fsdp')), may hold values from -6 to 6
- cotangent: bfloat16 [4096, 1280], P(('rep', 'fsdp')), may hold values from -1 to 1
- clip_lengths: int32 [4, 8], P('rep'), may hold values from 96 to 128, as said below
- group_clips: int32 [4], P('rep'), may hold values from 6 to 8, as said below
- outer_attention: float32 [2, 1280, 5120], P(None, 'fsdp')
- outer_feedforward: float32 [2, 1280, 10240], P(None, 'fsdp')
- outer_vectors: float32 [2, 12, 1280], P(None, None, 'fsdp')
- moments_attention: float32 [4, 2, 1280, 5120], P('rep', None, 'fsdp')
- moments_feedforward: float32 [4, 2, 1280, 10240], P('rep', None, 'fsdp')
- moments_vectors: float32 [4, 2, 12, 1280], P('rep', None, None, 'fsdp')
Outputs:
- block_output: bfloat16 [4096, 1280], P(('rep', 'fsdp'))
- input_grad: float32 [4096, 1280], P(('rep', 'fsdp'))
- group_attention: float32 [4, 3, 1280, 5120], P('rep', None, 'fsdp')
- group_feedforward: float32 [4, 3, 1280, 10240], P('rep', None, 'fsdp')
- group_vectors: float32 [4, 3, 12, 1280], P('rep', None, None, 'fsdp')
- group_weights: float32 [4, 1280, 15372], P('rep', 'fsdp')
- next_attention: float32 [3, 1280, 5120], P(None, 'fsdp')
- next_feedforward: float32 [3, 1280, 10240], P(None, 'fsdp')
- next_vectors: float32 [3, 12, 1280], P(None, None, 'fsdp')
- copy_attention: bfloat16 [1280, 5120], P('fsdp')
- copy_feedforward: bfloat16 [1280, 10240], P('fsdp')
- copy_vectors: bfloat16 [12, 1280], P(None, 'fsdp')
Inputs may be any that keep to these rules, and one draw needn't show every extreme that they name: `clip_lengths`: some clip has exactly 128 valid tokens and some exactly 96. Group g holds clips in its slots 0 to group_clips[g] - 1 and none in the others; some group has all 8 and some 8 - 2.
All inputs are finite; a program needn't handle non-finite values.
Results may differ from a plain program's by a relative error of at most 0.012.
The roundings to bfloat16 on the way count: a program that leaves them out, or rounds other values in their place, can miss the bound.
Values may be sent and summed in bfloat16 or wider, within the bound.
A program may use at most 448 MiB of HBM per device.

v0:
```python
from functools import partial
import jax
import jax.numpy as jnp
from jax import lax
from jax.sharding import PartitionSpec as P

D = 1280
HEADS = 16
HD = 80
FF = 5120
STEP = 3
NORM_EPS = 1e-05
MASKED = -1e30
ADAM_RATE = 0.03
ADAM_DECAY = 0.1
ADAM_BETA = 0.5
ADAM_EPS = 1e-08
OUTER_RATE = 0.7
OUTER_MOMENTUM = 0.5


def contract_last(left, right):
    return lax.dot_general(
        left, right, (((1,), (1,)), ((), ())), preferred_element_type=jnp.float32
    )


def contract_rows(left, right):
    return lax.dot_general(
        left, right, (((0,), (0,)), ((), ())), preferred_element_type=jnp.float32
    )


def normalize(inputs, gain_row, shift_row):
    average = jnp.mean(inputs, axis=-1, keepdims=True)
    centered = inputs - average
    reciprocal = lax.rsqrt(jnp.mean(centered * centered, axis=-1, keepdims=True) + NORM_EPS)
    unit_rows = centered * reciprocal
    return (unit_rows * gain_row + shift_row, unit_rows, reciprocal)


def normalize_back(incoming, unit_rows, reciprocal, gain_row):
    scaled = incoming * gain_row
    centered = scaled - jnp.mean(scaled, axis=-1, keepdims=True)
    return reciprocal * (
        centered - unit_rows * jnp.mean(scaled * unit_rows, axis=-1, keepdims=True)
    )


def adamw_step(weight, gradient, moments, decay_rate):
    first_moment = ADAM_BETA * moments[0] + (1.0 - ADAM_BETA) * gradient
    second_moment = ADAM_BETA * moments[1] + (1.0 - ADAM_BETA) * gradient * gradient
    correction = 1.0 - ADAM_BETA**STEP
    direction = first_moment / correction / (jnp.sqrt(second_moment / correction) + ADAM_EPS)
    return (weight - ADAM_RATE * (direction + decay_rate * weight), first_moment, second_moment)


def outer_step(master, mean_delta, momentum_old):
    momentum = OUTER_MOMENTUM * momentum_old - mean_delta
    outer_next = master - OUTER_RATE * (OUTER_MOMENTUM * momentum - mean_delta)
    return jnp.stack([mean_delta, momentum, outer_next])


def shards(
    features,
    cotangent,
    clip_lengths,
    group_clips,
    outer_attention,
    outer_feedforward,
    outer_vectors,
    moments_attention,
    moments_feedforward,
    moments_vectors,
):
    tokens_here = features.shape[0]
    scale = HD ** (-0.5)
    clip_slot = lax.axis_index("fsdp")
    clip_length = lax.dynamic_index_in_dim(clip_lengths[0], clip_slot, keepdims=False)
    live_clip = clip_slot < group_clips[0]
    positions = jnp.arange(tokens_here, dtype=jnp.int32)
    key_valid = positions < clip_length
    row_valid = key_valid & live_clip
    masters = (outer_attention[0], outer_feedforward[0], outer_vectors[0])
    copies = (
        masters[0].astype(jnp.bfloat16),
        masters[1].astype(jnp.bfloat16),
        masters[2].astype(jnp.bfloat16),
    )
    full_attention, full_feedforward, full_vectors = (
        lax.all_gather(copies[0], "fsdp", axis=0, tiled=True),
        lax.all_gather(copies[1], "fsdp", axis=0, tiled=True),
        lax.all_gather(copies[2], "fsdp", axis=1, tiled=True),
    )
    vectors = full_vectors.astype(jnp.float32)
    inputs = features.astype(jnp.float32)
    normed_one, unit_one, scale_one = normalize(inputs, vectors[0], vectors[1])
    layer_one = normed_one.astype(jnp.bfloat16)
    qkv_bias = jnp.concatenate([vectors[2], jnp.zeros_like(vectors[2]), vectors[3]])
    projected = (
        jnp.dot(layer_one, full_attention[:, : 3 * D], preferred_element_type=jnp.float32)
        + qkv_bias
    ).astype(jnp.bfloat16)
    query_heads = projected[:, :D].reshape(tokens_here, HEADS, HD)
    key_heads = projected[:, D : 2 * D].reshape(tokens_here, HEADS, HD)
    value_heads = projected[:, 2 * D :].reshape(tokens_here, HEADS, HD)

    def score_block():
        raw_scores = (
            jnp.einsum("qhd,khd->hqk", query_heads, key_heads, preferred_element_type=jnp.float32)
            * scale
        )
        return jnp.where(key_valid[None, None, :], raw_scores, MASKED)

    scores = score_block()
    top_score = jnp.max(scores, axis=-1, keepdims=True)
    exponent = jnp.exp(scores - top_score)
    totals = jnp.sum(exponent, axis=-1, keepdims=True)
    attention_probs = exponent / totals
    log_totals = top_score + jnp.log(totals)
    attended = jnp.einsum(
        "hqk,khd->qhd",
        attention_probs.astype(jnp.bfloat16),
        value_heads,
        preferred_element_type=jnp.float32,
    )
    attended = attended.reshape(tokens_here, D).astype(jnp.bfloat16)
    attention_branch = contract_last(attended, full_attention[:, 3 * D :]) + vectors[4]
    middle = inputs + attention_branch
    normed_two, unit_two, scale_two = normalize(middle, vectors[5], vectors[6])
    layer_two = normed_two.astype(jnp.bfloat16)
    pre_activation = jnp.dot(
        layer_two, full_feedforward[:, :FF], preferred_element_type=jnp.float32
    ) + vectors[8:].reshape(FF)
    activation, gelu_backward = jax.vjp(partial(jax.nn.gelu, approximate=False), pre_activation)
    activation_low = activation.astype(jnp.bfloat16)
    feedforward_branch = contract_last(activation_low, full_feedforward[:, FF:]) + vectors[7]
    block_output = (middle + feedforward_branch).astype(jnp.bfloat16)
    back_attention, back_feedforward, back_vectors = (
        lax.all_gather(copies[0], "fsdp", axis=0, tiled=True),
        lax.all_gather(copies[1], "fsdp", axis=0, tiled=True),
        lax.all_gather(copies[2], "fsdp", axis=1, tiled=True),
    )
    gain_rows = back_vectors.astype(jnp.float32)
    upstream = cotangent.astype(jnp.float32) * row_valid[:, None].astype(jnp.float32)
    upstream_low = upstream.astype(jnp.bfloat16)
    grad_down_bias = jnp.sum(upstream_low, axis=0, dtype=jnp.float32)
    grad_activation = jnp.dot(
        upstream_low, back_feedforward[:, FF:], preferred_element_type=jnp.float32
    )
    grad_pre = gelu_backward(grad_activation)[0].astype(jnp.bfloat16)
    grad_up_bias = jnp.sum(grad_pre, axis=0, dtype=jnp.float32)
    grad_two = contract_last(grad_pre, back_feedforward[:, :FF])
    grad_gain_two = jnp.sum(grad_two * unit_two, axis=0)
    grad_shift_two = jnp.sum(grad_two, axis=0)
    grad_middle = upstream + normalize_back(grad_two, unit_two, scale_two, gain_rows[5])
    middle_low = grad_middle.astype(jnp.bfloat16)
    grad_out_bias = jnp.sum(middle_low, axis=0, dtype=jnp.float32)
    grad_attended = jnp.dot(
        middle_low, back_attention[:, 3 * D :], preferred_element_type=jnp.float32
    ).astype(jnp.bfloat16)
    grad_heads = grad_attended.reshape(tokens_here, HEADS, HD)
    attention_probs = jnp.exp(score_block() - log_totals)
    grad_probs = jnp.einsum(
        "qhd,khd->hqk", grad_heads, value_heads, preferred_element_type=jnp.float32
    )
    row_dot = jnp.sum(attention_probs * grad_probs, axis=-1, keepdims=True)
    grad_scores = (attention_probs * (grad_probs - row_dot)).astype(jnp.bfloat16)
    grad_queries = (
        jnp.einsum("hqk,khd->qhd", grad_scores, key_heads, preferred_element_type=jnp.float32)
        * scale
    ).reshape(tokens_here, D)
    grad_keys = (
        jnp.einsum("hqk,qhd->khd", grad_scores, query_heads, preferred_element_type=jnp.float32)
        * scale
    ).reshape(tokens_here, D)
    grad_values = jnp.einsum(
        "hqk,qhd->khd",
        attention_probs.astype(jnp.bfloat16),
        grad_heads,
        preferred_element_type=jnp.float32,
    ).reshape(tokens_here, D)
    grad_qkv = jnp.concatenate([grad_queries, grad_keys, grad_values], axis=1).astype(jnp.bfloat16)
    grad_query_bias = jnp.sum(grad_qkv[:, :D], axis=0, dtype=jnp.float32)
    grad_value_bias = jnp.sum(grad_qkv[:, 2 * D :], axis=0, dtype=jnp.float32)
    grad_one = contract_last(grad_qkv, back_attention[:, : 3 * D])
    grad_gain_one = jnp.sum(grad_one * unit_one, axis=0)
    grad_shift_one = jnp.sum(grad_one, axis=0)
    input_grad = grad_middle + normalize_back(grad_one, unit_one, scale_one, gain_rows[0])
    vector_rows = jnp.stack(
        [
            grad_gain_one,
            grad_shift_one,
            grad_query_bias,
            grad_value_bias,
            grad_out_bias,
            grad_gain_two,
            grad_shift_two,
            grad_down_bias,
        ]
    )
    grad_vectors = jnp.concatenate([vector_rows, grad_up_bias.reshape(4, D)], axis=0)
    owned_attention = lax.psum_scatter(
        jnp.concatenate(
            [contract_rows(layer_one, grad_qkv), contract_rows(middle_low, attended)], axis=1
        ),
        "fsdp",
        scatter_dimension=0,
        tiled=True,
    )
    owned_feedforward = lax.psum_scatter(
        jnp.concatenate(
            [contract_rows(layer_two, grad_pre), contract_rows(upstream_low, activation_low)],
            axis=1,
        ),
        "fsdp",
        scatter_dimension=0,
        tiled=True,
    )
    owned_vectors = lax.psum_scatter(grad_vectors, "fsdp", scatter_dimension=1, tiled=True)
    new_attention, first_attention, second_attention = adamw_step(
        masters[0], owned_attention, moments_attention[0], ADAM_DECAY
    )
    new_feedforward, first_feedforward, second_feedforward = adamw_step(
        masters[1], owned_feedforward, moments_feedforward[0], ADAM_DECAY
    )
    new_vectors, first_vectors, second_vectors = adamw_step(
        masters[2], owned_vectors, moments_vectors[0], 0.0
    )
    summed = (
        lax.psum_scatter(
            (new_attention - masters[0]).astype(jnp.bfloat16),
            "rep",
            scatter_dimension=1,
            tiled=True,
        ).astype(jnp.float32),
        lax.psum_scatter(
            (new_feedforward - masters[1]).astype(jnp.bfloat16),
            "rep",
            scatter_dimension=1,
            tiled=True,
        ).astype(jnp.float32),
        lax.psum_scatter(
            (new_vectors - masters[2]).astype(jnp.bfloat16), "rep", scatter_dimension=0, tiled=True
        ).astype(jnp.float32),
    )
    replicas = lax.axis_size("rep")
    replica_index = lax.axis_index("rep")
    attention_cols = 4 * D // replicas
    feedforward_cols = 2 * FF // replicas
    vector_count = 12 // replicas

    def owned_part(array, dim, count):
        return lax.dynamic_slice_in_dim(array, replica_index * count, count, dim)

    part_attention = outer_step(
        owned_part(masters[0], 1, attention_cols),
        summed[0] / replicas,
        owned_part(outer_attention[1], 1, attention_cols),
    )
    part_feedforward = outer_step(
        owned_part(masters[1], 1, feedforward_cols),
        summed[1] / replicas,
        owned_part(outer_feedforward[1], 1, feedforward_cols),
    )
    part_vectors = outer_step(
        owned_part(masters[2], 0, vector_count),
        summed[2] / replicas,
        owned_part(outer_vectors[1], 0, vector_count),
    )
    next_attention, next_feedforward, next_vectors = (
        lax.all_gather(part_attention, "rep", axis=2, tiled=True),
        lax.all_gather(part_feedforward, "rep", axis=2, tiled=True),
        lax.all_gather(part_vectors, "rep", axis=1, tiled=True),
    )
    copy_attention = next_attention[2].astype(jnp.bfloat16)
    copy_feedforward = next_feedforward[2].astype(jnp.bfloat16)
    copy_vectors = next_vectors[2].astype(jnp.bfloat16)
    group_attention = jnp.stack([owned_attention, first_attention, second_attention])[None]
    group_feedforward = jnp.stack([owned_feedforward, first_feedforward, second_feedforward])[None]
    group_vectors = jnp.stack([owned_vectors, first_vectors, second_vectors])[None]
    group_weights = jnp.concatenate([new_attention, new_feedforward, new_vectors.T], axis=1)[None]
    return (
        block_output,
        input_grad,
        group_attention,
        group_feedforward,
        group_vectors,
        group_weights,
        next_attention,
        next_feedforward,
        next_vectors,
        copy_attention,
        copy_feedforward,
        copy_vectors,
    )


def solution(mesh):
    in_specs = (
        P(("rep", "fsdp"), None),
        P(("rep", "fsdp"), None),
        P("rep", None),
        P("rep"),
        P(None, "fsdp", None),
        P(None, "fsdp", None),
        P(None, None, "fsdp"),
        P("rep", None, "fsdp", None),
        P("rep", None, "fsdp", None),
        P("rep", None, None, "fsdp"),
    )
    out_specs = (
        P(("rep", "fsdp"), None),
        P(("rep", "fsdp"), None),
        P("rep", None, "fsdp", None),
        P("rep", None, "fsdp", None),
        P("rep", None, None, "fsdp"),
        P("rep", "fsdp", None),
        P(None, "fsdp", None),
        P(None, "fsdp", None),
        P(None, None, "fsdp"),
        P("fsdp", None),
        P("fsdp", None),
        P(None, "fsdp"),
    )
    return jax.shard_map(shards, mesh=mesh, in_specs=in_specs, out_specs=out_specs, check_vma=False)
```

profile of v0, /device:TPU:0, one launch (start us, length us, event | category | flops | bytes accessed | tf_op | source)
XLA Modules:
  0.0 2351.6 jit_solution(7769149582330624274)
XLA Ops:
  7.2 3.3 bitcast_convert_fusion.1
  10.6 5.0 bitcast_convert_fusion
  17.1 33.6 %all-gather = bf16[8,160,12]{1,2,0:T(8,128)(2,1)S(1)} all-gather(bf16[1,160,12]{1,2,0:T(8,128)(2,1)S(1)} %copy.142), channel_id=1, replica_groups=mesh['rep'=4,'fsdp'=8] {'fsdp'}, dimensions={0}, use_global_device_ids=true | all-gather | bytes 34560 | tf_op jit(solution)/shard_map/all_gather | solution.py:93
  54.6 141.9 %all-gather.6.cloned.1.call-done = bf16[1280,5120]{1,0:T(8,128)(2,1)} async-done(((bf16[160,5120]{1,0:T(8,128)(2,1)}), bf16[1280,5120]{1,0:T(8,128)(2,1)}) %all-gather.6.cloned.1.call-update) | async-done | bytes 13107216 | tf_op jit(solution)/shard_map/all_gather | solution.py:91
  196.5 5.3 fusion.22
  203.5 3.7 fusion.122
  207.5 489.4 %all-gather.8.cloned.1.call-done = bf16[1280,10240]{1,0:T(8,128)(2,1)} async-done(((bf16[160,10240]{1,0:T(8,128)(2,1)}), bf16[1280,10240]{1,0:T(8,128)(2,1)}) %all-gather.8.cloned.1.call-update) | async-done | bytes 26214416 | tf_op jit(solution)/shard_map/all_gather | solution.py:92
  696.8 5.9 fusion.16
  702.8 11.3 convert_reduce_fusion
  714.1 8.4 multiply_reduce_fusion.1
  723.0 3.3 fusion.57
  726.2 1.9 copy.148
  728.1 1.5 convolution_convert_fusion
  729.6 1.6 multiply_reduce_fusion
  732.3 1.0 fusion.107
  733.3 2.9 fusion.93
  736.2 9.2 pad_maximum_fusion.1
  745.6 13.1 fusion.115
  758.6 12.3 fusion.110
  770.9 34.1 %pad_maximum_fusion = f32[1280,10240]{1,0:T(8,128)} fusion(f32[1280,5120]{1,0:T(8,128)} %fusion.110, f32[1280,5120]{1,0:T(8,128)} %fusion.115), kind=kLoop, calls=%fused_computation | loop fusion | flops 13107200 | bytes 104857600 | tf_op jit(solution)/shard_map/concatenate | solution.py:212
  805.1 358.9 %reduce-scatter.7.cloned.1.call-done = f32[160,5120]{1,0:T(8,128)} async-done(((f32[1280,5120]{1,0:T(8,128)}), f32[160,5120]{1,0:T(8,128)}) %reduce-scatter.7.cloned.1.call-update) | async-done | bytes 3276816 | tf_op jit(solution)/shard_map/reduce_scatter | solution.py:203
  1164.0 9.6 fusion.29
  1173.7 811.0 %reduce-scatter.9.cloned.1.call-done = f32[160,10240]{1,0:T(8,128)} async-done(((f32[1280,10240]{1,0:T(8,128)}), f32[160,10240]{1,0:T(8,128)}) %reduce-scatter.9.cloned.1.call-update) | async-done | bytes 6553616 | tf_op jit(solution)/shard_map/reduce_scatter | solution.py:211
  1984.6 18.2 fusion.15
  2003.2 6.5 fusion.117
  2009.7 6.0 fusion.87
  2016.3 1.1 copy.153
  2017.6 1.7 fusion.90
  2019.3 1.7 pad_maximum_fusion.3
  2021.1 12.6 fusion.116
  2033.6 22.6 reduce-scatter.15.cloned.1.call-done
  2056.3 2.8 fusion.66
  2059.1 2.5 pad_maximum_fusion.2
  2065.3 1.1 fusion.86
  2066.4 13.2 fusion.54
  2079.6 42.7 %reduce-scatter.11.cloned.1.call-done = f32[12,160]{0,1:T(8,128)} async-done(((f32[12,1280]{0,1:T(8,128)}), f32[12,160]{0,1:T(8,128)}) %reduce-scatter.11.cloned.1.call-update) | async-done | bytes 7696 | tf_op jit(solution)/shard_map/reduce_scatter | solution.py:220
  2122.3 1.7 fusion.98
  2127.6 12.0 all-reduce
  2139.9 5.8 all_gather.26
  2146.3 8.3 maximum_bitcast_fusion.2
  2154.6 35.4 %all-gather.10.cloned.1.call-done = f32[3,160,5120]{2,1,0:T(8,128)} async-done(((f32[3,160,1280]{2,1,0:T(8,128)}), f32[3,160,5120]{2,1,0:T(8,128)}) %all-gather.10.cloned.1.call-update) | async-done | bytes 9830416 | tf_op jit(solution)/shard_map/all_gather | solution.py:272
  2190.0 3.3 fusion.61
  2193.4 19.0 maximum_bitcast_fusion
  2213.1 5.5 maximum_bitcast_fusion.1
  2218.6 97.3 %all-gather.12.cloned.1.call-done = f32[3,160,10240]{2,1,0:T(8,128)} async-done(((f32[3,160,2560]{2,1,0:T(8,128)}), f32[3,160,10240]{2,1,0:T(8,128)}) %all-gather.12.cloned.1.call-update) | async-done | bytes 19660816 | tf_op jit(solution)/shard_map/all_gather | solution.py:273
  2315.8 5.0 fusion.26
  2320.8 8.8 copy.180
  2329.6 15.0 copy.181
  (134 shorter events, 17.4 us)
Async XLA Ops:
  7.2 44.4 %copy-start = (s32[1,8]{1,0:T(1,128)S(1)}, s32[1,8]{1,0:T(1,128)}, u32[]{:S(2)}) copy-start(s32[1,8]{1,0:T(1,128)} %param.12) | copy-start | bytes 100
  7.2 189.3 %all-gather.6.cloned.1.call-start = ((), (), s32[]{:S(2)}) async-start(), calls=%async_computation.5 | async-start | bytes 14745600 | tf_op jit(solution)/shard_map/all_gather | solution.py:91
  10.6 686.3 %all-gather.8.cloned.1.call-start = ((), (), s32[]{:S(2)}) async-start(), calls=%async_computation.6 | async-start | bytes 29491200 | tf_op jit(solution)/shard_map/all_gather | solution.py:92
  15.6 0.7 copy-start.17
  15.6 38.6 %copy-start.5 = (bf16[128,1280]{1,0:T(8,128)(2,1)S(1)}, bf16[128,1280]{1,0:T(8,128)(2,1)}, u32[]{:S(2)}) copy-start(bf16[128,1280]{1,0:T(8,128)(2,1)} %param.10) | copy-start | bytes 983044
  15.6 1148.4 %reduce-scatter.7.cloned.1.call-start = ((), (), s32[]{:S(2)}) async-start(), calls=%async_computation.7 | async-start | bytes 29491200 | tf_op jit(solution)/shard_map/reduce_scatter | solution.py:203
  17.1 184.8 %copy-start.9 = (f32[1,12,160]{1,2,0:T(8,128)}, f32[1,12,160]{1,2,0:T(8,128)S(1)}, u32[]{:S(2)}) copy-start(f32[1,12,160]{1,2,0:T(8,128)S(1)} %copy.171) | copy-start | bytes 23044
  202.1 1.3 copy-start.11
  203.5 3.7 copy-start.12
  207.2 538.3 %copy-start.4 = (f32[128,1280]{1,0:T(8,128)}, f32[128,1280]{1,0:T(8,128)S(1)}, u32[]{:S(2)}) copy-start(f32[128,1280]{1,0:T(8,128)S(1)} %get-tuple-element.138) | copy-start | bytes 1966084
  696.8 5.9 copy-start.14
  702.8 11.3 copy-start.21
  714.1 8.4 copy-start.8
  729.6 3.7 copy-start.6
  731.2 1.1 copy-start.13
  745.5 13.2 copy-start.15
  745.5 1239.1 %reduce-scatter.9.cloned.1.call-start = ((), (), s32[]{:S(2)}) async-start(), calls=%async_computation.8 | async-start | bytes 58982400 | tf_op jit(solution)/shard_map/reduce_scatter | solution.py:211
  745.5 13.1 copy-start.22
  805.0 1212.5 %reduce-scatter.13.cloned.1.call-start = ((), (), s32[]{:S(2)}) async-start(), calls=%async_computation.10 | async-start | bytes 2048000 | tf_op jit(solution)/shard_map/reduce_scatter | solution.py:231
  1173.6 882.6 %reduce-scatter.15.cloned.1.call-start = ((), (), s32[]{:S(2)}) async-start(), calls=%async_computation.12 | async-start | bytes 4096000 | tf_op jit(solution)/shard_map/reduce_scatter | solution.py:237
  2002.9 119.4 %reduce-scatter.11.cloned.1.call-start = ((), (), s32[]{:S(2)}) async-start(), calls=%async_computation.9 | async-start | bytes 737280 | tf_op jit(solution)/shard_map/reduce_scatter | solution.py:220
  2003.2 6.5 copy-start.7
  2017.5 172.6 %all-gather.10.cloned.1.call-start = ((), (), s32[]{:S(2)}) async-start(), calls=%async_computation.11 | async-start | bytes 12288000 | tf_op jit(solution)/shard_map/all_gather | solution.py:272
  2021.0 294.8 %all-gather.12.cloned.1.call-start = ((), (), s32[]{:S(2)}) async-start(), calls=%async_computation.13 | async-start | bytes 24576000 | tf_op jit(solution)/shard_map/all_gather | solution.py:273
  2061.6 0.7 copy-start.18
  2061.6 2.4 copy-start.20
  2061.6 4.8 copy-start.19
  2066.4 55.9 %copy-start.10 = (f32[1,12,160]{1,2,0:T(8,128)S(1)}, f32[1,12,160]{1,2,0:T(8,128)}, u32[]{:S(2)}) copy-start(f32[1,12,160]{1,2,0:T(8,128)} %copy-done.9) | copy-start | bytes 23044
  2066.4 79.9 %copy-start.2 = (f32[160,5120]{1,0:T(8,128)S(1)}, f32[160,5120]{1,0:T(8,128)}, u32[]{:S(2)}) copy-start(f32[160,5120]{1,0:T(8,128)} %reduce-scatter.7.cloned.1.call-done) | copy-start | bytes 9830404
  2145.7 9.0 copy-start.16
  2193.3 19.0 slice-start
  2193.3 19.0 slice-start.1
  2193.3 19.7 copy-start.3
  2329.6 15.0 copy-start.1
Sparse Core Ops, SparseCore 0:
  10.8 185.6 all-gather.5
  198.6 498.2 all-gather.7
  745.6 418.3 reduce-scatter.6
  1167.8 816.8 reduce-scatter.8
  1987.6 27.6 reduce-scatter.12
  2017.7 38.5 reduce-scatter.14
  2059.5 62.7 reduce-scatter.10
  2123.9 66.1 all-gather.9
  2191.6 124.1 all-gather.11
where the time goes:
time: 2360 us; the launch traced here: 2350 us
  waiting for transfers between devices  2000 us (85%)
  other arithmetic  119 us (5%)
  matrix products  91.1 us (4%)
  local copies, waits for them, and re-layouts  74.3 us (3%)
  blocking collectives  51.4 us (2%)
    reduce_scatter x1, waiting for transfers between devices, shards(): lax.psum_scatter(jnp.concatenate([contract_rows(layer_two, grad_pre), con...  811 us
    all_gather x1, waiting for transfers between devices, shards(): lax.all_gather(copies[1], 'fsdp', axis=0, tiled=True)  489 us
    reduce_scatter x1, waiting for transfers between devices, shards(): lax.psum_scatter(jnp.concatenate([contract_rows(layer_one, grad_qkv), con...  359 us
    all_gather x1, waiting for transfers between devices, shards(): lax.all_gather(copies[0], 'fsdp', axis=0, tiled=True)  142 us
    all_gather x1, waiting for transfers between devices, shards(): lax.all_gather(part_feedforward, 'rep', axis=2, tiled=True)  97.3 us
  transfers between devices with their start and end apart: 9, of which 8 were waited for; matrix products, arithmetic and copies ran while one was open for 9% of the time, Pallas kernels for 0%

commit v1 on v0

--- a/solution.py
+++ b/solution.py
@@ -17,6 +17,22 @@
 ADAM_EPS = 1e-08
 OUTER_RATE = 0.7
 OUTER_MOMENTUM = 0.5
+
+
+def ring_gather(x, axis, dim):
+    ways, here, step = (lax.axis_size(axis), lax.axis_index(axis), x.shape[dim])
+    shape = [n * ways if d == dim else n for d, n in enumerate(x.shape)]
+    full = lax.dynamic_update_slice_in_dim(jnp.zeros(shape, x.dtype), x, here * step, axis=dim)
+    going_up = going_down = x
+    for far in range(1, ways // 2 + 1):
+        going_up = lax.ppermute(going_up, axis, [(d, (d + 1) % ways) for d in range(ways)])
+        full = lax.dynamic_update_slice_in_dim(full, going_up, (here - far) % ways * step, axis=dim)
+        if 2 * far < ways:
+            going_down = lax.ppermute(going_down, axis, [(d, (d - 1) % ways) for d in range(ways)])
+            full = lax.dynamic_update_slice_in_dim(
+                full, going_down, (here + far) % ways * step, axis=dim
+            )
+    return full
 
 
 def contract_last(left, right):
@@ -270,7 +286,7 @@
     )
     next_attention, next_feedforward, next_vectors = (
         lax.all_gather(part_attention, "rep", axis=2, tiled=True),
-        lax.all_gather(part_feedforward, "rep", axis=2, tiled=True),
+        ring_gather(part_feedforward, "rep", 2),
         lax.all_gather(part_vectors, "rep", axis=1, tiled=True),
     )
     copy_attention = next_attention[2].astype(jnp.bfloat16)

time: 2360 us -> 2330 us (0.987)
  waiting for transfers between devices: 2000 us -> 1960 us
    all_gather x1 -> x0, waiting for transfers between devices: 97.3 us -> none  [shards(): lax.all_gather(part_feedforward, 'rep', axis=2, tiled=True)]
    ppermute x0 -> x3, waiting for transfers between devices: none -> 41.3 us  [the longest x1 41.3 us: ring_gather(): lax.ppermute(going_down, axis, [(d, (d - 1) % ways) for d in range(ways)])]
    all_gather x1, waiting for transfers between devices: 35.4 us -> 62.8 us  [shards(): lax.all_gather(part_attention, 'rep', axis=2, tiled=True)]
  transfers between devices with their start and end apart: 9 -> 11, of which waited for: 8 -> 8; matrix products, arithmetic and copies ran while one was open for 9% -> 9% of each run, Pallas kernels for 0% -> 0%
where the time goes in v1:
time: 2330 us; the launch traced here: 2320 us
  waiting for transfers between devices  1960 us (84%)
  other arithmetic  120 us (5%)
  matrix products  89.2 us (4%)
  local copies, waits for them, and re-layouts  79 us (3%)
  blocking collectives  51.2 us (2%)
    reduce_scatter x1, waiting for transfers between devices, shards(): lax.psum_scatter(jnp.concatenate([contract_rows(layer_two, grad_pre), con...  811 us
    all_gather x1, waiting for transfers between devices, shards(): lax.all_gather(copies[1], 'fsdp', axis=0, tiled=True)  489 us
    reduce_scatter x1, waiting for transfers between devices, shards(): lax.psum_scatter(jnp.concatenate([contract_rows(layer_one, grad_qkv), con...  359 us
    all_gather x1, waiting for transfers between devices, shards(): lax.all_gather(copies[0], 'fsdp', axis=0, tiled=True)  142 us
    all_gather x1, waiting for transfers between devices, shards(): lax.all_gather(part_attention, 'rep', axis=2, tiled=True)  62.8 us
  transfers between devices with their start and end apart: 11, of which 8 were waited for; matrix products, arithmetic and copies ran while one was open for 9% of the time, Pallas kernels for 0%

profile of v1, /device:TPU:0, one launch (start us, length us, event | category | flops | bytes accessed | tf_op | source)
XLA Modules:
  0.0 2318.0 jit_solution(4520872108890022459)
XLA Ops:
  7.2 3.3 bitcast_convert_fusion.1
  10.6 5.0 bitcast_convert_fusion
  17.1 33.6 %all-gather = bf16[8,160,12]{1,2,0:T(8,128)(2,1)S(1)} all-gather(bf16[1,160,12]{1,2,0:T(8,128)(2,1)S(1)} %copy.142), channel_id=1, replica_groups=mesh['rep'=4,'fsdp'=8] {'fsdp'}, dimensions={0}, use_global_device_ids=true | all-gather | bytes 34560 | tf_op jit(solution)/shard_map/all_gather | solution.py:109
  54.6 141.9 %all-gather.5.cloned.1.call-done = bf16[1280,5120]{1,0:T(8,128)(2,1)} async-done(((bf16[160,5120]{1,0:T(8,128)(2,1)}), bf16[1280,5120]{1,0:T(8,128)(2,1)}) %all-gather.5.cloned.1.call-update) | async-done | bytes 13107216 | tf_op jit(solution)/shard_map/all_gather | solution.py:107
  196.5 5.3 fusion.22
  203.5 3.7 fusion.122
  207.5 489.4 %all-gather.7.cloned.1.call-done = bf16[1280,10240]{1,0:T(8,128)(2,1)} async-done(((bf16[160,10240]{1,0:T(8,128)(2,1)}), bf16[1280,10240]{1,0:T(8,128)(2,1)}) %all-gather.7.cloned.1.call-update) | async-done | bytes 26214416 | tf_op jit(solution)/shard_map/all_gather | solution.py:108
  696.8 5.9 fusion.16
  702.8 11.3 convert_reduce_fusion
  714.1 8.4 multiply_reduce_fusion.1
  723.0 3.5 fusion.57
  726.5 1.9 copy.148
  729.8 1.6 multiply_reduce_fusion
  733.6 2.9 fusion.93
  736.5 9.2 pad_maximum_fusion.1
  747.0 11.6 fusion.115
  758.6 12.3 fusion.110
  770.9 34.3 %pad_maximum_fusion = f32[1280,10240]{1,0:T(8,128)} fusion(f32[1280,5120]{1,0:T(8,128)} %fusion.110, f32[1280,5120]{1,0:T(8,128)} %fusion.115), kind=kLoop, calls=%fused_computation | loop fusion | flops 13107200 | bytes 104857600 | tf_op jit(solution)/shard_map/concatenate | solution.py:228
  805.3 358.9 %reduce-scatter.7.cloned.1.call-done = f32[160,5120]{1,0:T(8,128)} async-done(((f32[1280,5120]{1,0:T(8,128)}), f32[160,5120]{1,0:T(8,128)}) %reduce-scatter.7.cloned.1.call-update) | async-done | bytes 3276816 | tf_op jit(solution)/shard_map/reduce_scatter | solution.py:219
  1164.1 9.6 fusion.29
  1173.8 810.6 %reduce-scatter.9.cloned.1.call-done = f32[160,10240]{1,0:T(8,128)} async-done(((f32[1280,10240]{1,0:T(8,128)}), f32[160,10240]{1,0:T(8,128)}) %reduce-scatter.9.cloned.1.call-update) | async-done | bytes 6553616 | tf_op jit(solution)/shard_map/reduce_scatter | solution.py:227
  1984.4 18.2 fusion.15
  2003.0 6.5 fusion.117
  2009.5 6.0 fusion.87
  2017.3 1.7 fusion.90
  2019.1 1.7 pad_maximum_fusion.3
  2023.8 12.3 fusion.116
  2036.1 19.9 reduce-scatter.15.cloned.1.call-done
  2055.9 2.8 fusion.66
  2058.8 9.5 broadcast_in_dim.56
  2068.3 5.1 pad_maximum_fusion.2
  2074.6 12.6 fusion.54
  2087.1 34.8 %reduce-scatter.11.cloned.1.call-done = f32[12,160]{0,1:T(8,128)} async-done(((f32[12,1280]{0,1:T(8,128)}), f32[12,160]{0,1:T(8,128)}) %reduce-scatter.11.cloned.1.call-update) | async-done | bytes 7696 | tf_op jit(solution)/shard_map/reduce_scatter | solution.py:236
  2121.9 1.7 fusion.98
  2127.2 12.0 all-reduce
  2139.6 5.5 all_gather.22
  2145.7 8.3 maximum_bitcast_fusion.2
  2154.1 2.1 collective-permute-start.1
  2156.4 62.8 %all-gather.9.cloned.1.call-done = f32[3,160,5120]{2,1,0:T(8,128)} async-done(((f32[3,160,1280]{2,1,0:T(8,128)}), f32[3,160,5120]{2,1,0:T(8,128)}) %all-gather.9.cloned.1.call-update) | async-done | bytes 9830416 | tf_op jit(solution)/shard_map/all_gather | solution.py:288
  2219.2 3.3 fusion.61
  2222.5 17.0 maximum_bitcast_fusion
  2239.5 5.5 maximum_bitcast_fusion.1
  2245.0 5.0 constant_dynamic-update-slice_fusion.2
  2249.9 41.3 %collective-permute-done.1 = f32[3,160,2560]{2,1,0:T(8,128)} collective-permute-done((f32[3,160,2560]{2,1,0:T(8,128)}, f32[3,160,2560]{2,1,0:T(8,128)}, u32[]{:S(2)}, u32[]{:S(2)}) %collective-permute-start.1) | collective-permute-done | bytes 4915232 | tf_op jit(solution)/shard_map/ppermute | solution.py:31
  2291.2 5.4 constant_dynamic-update-slice_fusion.1
  2296.6 5.3 constant_dynamic-update-slice_fusion
  2301.9 5.0 fusion.26
  2306.9 3.9 copy.183
  (161 shorter events, 22.1 us)
Async XLA Ops:
  7.2 44.4 %copy-start = (s32[1,8]{1,0:T(1,128)S(1)}, s32[1,8]{1,0:T(1,128)}, u32[]{:S(2)}) copy-start(s32[1,8]{1,0:T(1,128)} %param.12) | copy-start | bytes 100
  7.2 189.3 %all-gather.5.cloned.1.call-start = ((), (), s32[]{:S(2)}) async-start(), calls=%async_computation.5 | async-start | bytes 14745600 | tf_op jit(solution)/shard_map/all_gather | solution.py:107
  10.6 686.3 %all-gather.7.cloned.1.call-start = ((), (), s32[]{:S(2)}) async-start(), calls=%async_computation.6 | async-start | bytes 29491200 | tf_op jit(solution)/shard_map/all_gather | solution.py:108
  15.6 0.7 copy-start.23
  15.6 38.6 %copy-start.8 = (bf16[128,1280]{1,0:T(8,128)(2,1)S(1)}, bf16[128,1280]{1,0:T(8,128)(2,1)}, u32[]{:S(2)}) copy-start(bf16[128,1280]{1,0:T(8,128)(2,1)} %param.10) | copy-start | bytes 983044
  15.6 1148.5 %reduce-scatter.7.cloned.1.call-start = ((), (), s32[]{:S(2)}) async-start(), calls=%async_computation.7 | async-start | bytes 29491200 | tf_op jit(solution)/shard_map/reduce_scatter | solution.py:219
  17.1 184.8 %copy-start.13 = (f32[1,12,160]{1,2,0:T(8,128)}, f32[1,12,160]{1,2,0:T(8,128)S(1)}, u32[]{:S(2)}) copy-start(f32[1,12,160]{1,2,0:T(8,128)S(1)} %copy.171) | copy-start | bytes 23044
  202.1 1.3 copy-start.15
  203.5 3.7 copy-start.18
  207.2 538.6 %copy-start.6 = (f32[128,1280]{1,0:T(8,128)}, f32[128,1280]{1,0:T(8,128)S(1)}, u32[]{:S(2)}) copy-start(f32[128,1280]{1,0:T(8,128)S(1)} %get-tuple-element.140) | copy-start | bytes 1966084
  696.8 5.9 copy-start.20
  702.8 11.3 copy-start.27
  714.1 8.4 copy-start.11
  723.0 9.5 copy-start.4
  729.8 3.8 copy-start.9
  731.4 1.1 copy-start.19
  732.2 1.4 copy-start.16
  745.7 1.3 copy-start.12
  745.7 12.9 copy-start.21
  745.8 1238.6 %reduce-scatter.9.cloned.1.call-start = ((), (), s32[]{:S(2)}) async-start(), calls=%async_computation.8 | async-start | bytes 58982400 | tf_op jit(solution)/shard_map/reduce_scatter | solution.py:227
  747.0 11.6 copy-start.28
  805.2 1212.1 %reduce-scatter.13.cloned.1.call-start = ((), (), s32[]{:S(2)}) async-start(), calls=%async_computation.10 | async-start | bytes 2048000 | tf_op jit(solution)/shard_map/reduce_scatter | solution.py:247
  1173.8 882.2 %reduce-scatter.15.cloned.1.call-start = ((), (), s32[]{:S(2)}) async-start(), calls=%async_computation.12 | async-start | bytes 4096000 | tf_op jit(solution)/shard_map/reduce_scatter | solution.py:253
  2002.7 119.2 %reduce-scatter.11.cloned.1.call-start = ((), (), s32[]{:S(2)}) async-start(), calls=%async_computation.9 | async-start | bytes 737280 | tf_op jit(solution)/shard_map/reduce_scatter | solution.py:236
  2002.9 6.5 copy-start.10
  2003.0 6.5 copy-start.17
  2017.2 201.9 %all-gather.9.cloned.1.call-start = ((), (), s32[]{:S(2)}) async-start(), calls=%async_computation.11 | async-start | bytes 12288000 | tf_op jit(solution)/shard_map/all_gather | solution.py:288
  2019.1 1.8 copy-start.24
  2020.7 1.8 copy-start.26
  2068.3 5.1 copy-start.5
  2068.3 6.2 copy-start.7
  2068.3 6.2 copy-start.25
  2068.3 6.2 copy-start.29
  2073.4 82.7 %collective-permute-start = (f32[3,160,2560]{2,1,0:T(8,128)}, f32[3,160,2560]{2,1,0:T(8,128)}, u32[]{:S(2)}, u32[]{:S(2)}) collective-permute-start(f32[3,160,2560]{2,1,0:T(8,128)} %get-tuple-element.118), channel_id=1, source_target_pairs={{0,8},{8,16},{16,24},{24,0},{1,9},{9,17},{17,25},{25,1},{2,10},{10... | collective-permute-start | bytes 14745608 | tf_op jit(solution)/shard_map/ppermute | solution.py:28
  2074.5 47.4 %copy-start.14 = (f32[1,12,160]{1,2,0:T(8,128)S(1)}, f32[1,12,160]{1,2,0:T(8,128)}, u32[]{:S(2)}) copy-start(f32[1,12,160]{1,2,0:T(8,128)} %copy-done.13) | copy-start | bytes 23044
  2074.5 71.2 %copy-start.2 = (f32[160,5120]{1,0:T(8,128)S(1)}, f32[160,5120]{1,0:T(8,128)}, u32[]{:S(2)}) copy-start(f32[160,5120]{1,0:T(8,128)} %reduce-scatter.7.cloned.1.call-done) | copy-start | bytes 9830404
  2145.1 9.0 copy-start.22
  2154.1 137.1 %collective-permute-start.1 = (f32[3,160,2560]{2,1,0:T(8,128)}, f32[3,160,2560]{2,1,0:T(8,128)}, u32[]{:S(2)}, u32[]{:S(2)}) collective-permute-start(f32[3,160,2560]{2,1,0:T(8,128)} %get-tuple-element.118), channel_id=1, source_target_pairs={{0,24},{8,0},{16,8},{24,16},{1,25},{9,1},{17,9},{25,17},{2,26},{10... | collective-permute-start | bytes 14745608 | tf_op jit(solution)/shard_map/ppermute | solution.py:31
  2156.1 140.4 %collective-permute-start.2 = (f32[3,160,2560]{2,1,0:T(8,128)}, f32[3,160,2560]{2,1,0:T(8,128)}, u32[]{:S(2)}, u32[]{:S(2)}) collective-permute-start(f32[3,160,2560]{2,1,0:T(8,128)} %collective-permute-done), channel_id=1, source_target_pairs={{0,8},{8,16},{16,24},{24,0},{1,9},{9,17},{17,25},{25,1},{2,10},{10... | collective-permute-start | bytes 14745608 | tf_op jit(solution)/shard_map/ppermute | solution.py:28
  2222.5 17.0 slice-start
  2222.5 17.0 slice-start.1
  2222.5 17.0 copy-start.3
  2291.2 15.6 slice-start.2
  2291.2 15.6 slice-start.3
  2296.6 10.3 slice-start.4
  2306.9 3.9 copy-start.1
Sparse Core Ops, SparseCore 0:
  10.8 185.6 all-gather.4
  198.6 498.2 all-gather.6
  745.9 418.2 reduce-scatter.6
  1167.9 816.4 reduce-scatter.8
  1987.4 27.5 reduce-scatter.12
  2017.3 38.5 reduce-scatter.14
  2059.2 62.6 reduce-scatter.10
  2123.5 95.6 all-gather.8
